TPU v7x, 8 devices: a whole 2x2x1 slice. The times are simulated.
8 devices in a mesh: dp: 2 (over z, y), tp: 4 (over x, core).
Axes of the slice: x: 2, y: 2, z: 1, core: 2. Of those that a mesh axis runs over, the one named last changes fastest.
Arguments:
- tokens: bfloat16 [4, 64, 4096], P('dp'), parts along dimension 0
- seq_lens: int32 [4], P('dp'), parts along dimension 0
- w_q: bfloat16 [4096, 4096], P(None, 'tp')
- w_k: bfloat16 [4096, 4096], P(None, 'tp')
- w_v: bfloat16 [4096, 4096], P(None, 'tp')
- w_o: bfloat16 [4096, 4096], P('tp')
- g_q: bfloat16 [4096], P('tp')
- g_k: bfloat16 [4096], P('tp')
- g_attn: bfloat16 [4096], replicated
- g_mlp: bfloat16 [4096], replicated
- w_gate: bfloat16 [4096, 11008], P(None, 'tp')
- w_up: bfloat16 [4096, 11008], P(None, 'tp')
- w_down: bfloat16 [11008, 4096], P('tp')
Outputs:
- output 1: bfloat16 [4, 64, 4096], P('dp'), parts along dimension 0
- output 2: bfloat16 [4, 32, 64, 128], P('dp', 'tp'), parts along dimension 0
- output 3: bfloat16 [4, 32, 64, 128], P('dp', 'tp'), parts along dimension 0
There are 2 independent parts. A program takes and returns all parts, laid end to end along the dimension named above; an argument that names none is the same for every part.
All inputs are finite; a program needn't handle non-finite values.
Results may differ from a plain program's by a relative error of at most 0.0144316.
Values are sent between devices in bfloat16 or wider.
A program may use at most 1 GiB of HBM per device.

v0:
```python
import jax
import jax.numpy as jnp
from jax import lax
from jax.sharding import PartitionSpec as P

HEAD_DIM = 128
ROPE_BASE = 500000.0
NORM_EPS = 1e-6


def rope_tables(seq_len, head_dim):
    half_dim = head_dim // 2
    inv_freq = ROPE_BASE ** (-2.0 * jnp.arange(half_dim, dtype=jnp.float32) / head_dim)
    angles = jnp.arange(seq_len, dtype=jnp.float32)[:, None] * inv_freq[None, :]
    angles = jnp.concatenate([angles, angles], axis=-1)
    return jnp.cos(angles), jnp.sin(angles)


def apply_rope(vecs, cos_tab, sin_tab, head_axes):
    half_dim = vecs.shape[-1] // 2
    table_shape = (cos_tab.shape[0],) + (1,) * head_axes + (cos_tab.shape[1],)
    rotated = jnp.concatenate([-vecs[..., half_dim:], vecs[..., :half_dim]], axis=-1)
    return vecs * cos_tab.reshape(table_shape) + rotated * sin_tab.reshape(table_shape)


def rms_scale(vals):
    return lax.rsqrt(jnp.mean(vals * vals, axis=-1, keepdims=True) + NORM_EPS)


def post_norm(base, branch, gain):
    branch32 = branch.astype(jnp.float32)
    return (base.astype(jnp.float32) + branch32 * rms_scale(branch32) * gain.astype(jnp.float32)).astype(jnp.bfloat16)


def solution(mesh):
    tp_size = mesh.shape['tp']

    def local_layer(tokens, seq_lens, w_q, w_k, w_v, w_o, g_q, g_k, g_attn, g_mlp, w_gate, w_up, w_down):
        prompts, seq_len = tokens.shape[0], tokens.shape[1]
        kv_local = w_k.shape[1] // HEAD_DIM
        group_size = w_q.shape[1] // w_k.shape[1]
        q_raw = jnp.einsum('bsd,dn->bsn', tokens, w_q, preferred_element_type=jnp.float32)
        k_raw = jnp.einsum('bsd,dn->bsn', tokens, w_k, preferred_element_type=jnp.float32)
        v_new = jnp.einsum('bsd,dn->bsn', tokens, w_v, preferred_element_type=jnp.float32).astype(jnp.bfloat16)
        q_sumsq = lax.psum(jnp.sum(q_raw * q_raw, axis=-1, keepdims=True), 'tp')
        k_sumsq = lax.psum(jnp.sum(k_raw * k_raw, axis=-1, keepdims=True), 'tp')
        q_norm = q_raw * lax.rsqrt(q_sumsq / (w_q.shape[1] * tp_size) + NORM_EPS) * g_q.astype(jnp.float32)
        k_norm = k_raw * lax.rsqrt(k_sumsq / (w_k.shape[1] * tp_size) + NORM_EPS) * g_k.astype(jnp.float32)
        cos_tab, sin_tab = rope_tables(seq_len, HEAD_DIM)
        queries = apply_rope(q_norm.reshape(prompts, seq_len, kv_local, group_size, HEAD_DIM), cos_tab, sin_tab, 2).astype(jnp.bfloat16)
        keys_new = apply_rope(k_norm.reshape(prompts, seq_len, kv_local, HEAD_DIM), cos_tab, sin_tab, 1).astype(jnp.bfloat16)
        k_cache = jnp.transpose(keys_new, (0, 2, 1, 3))
        v_cache = jnp.transpose(v_new.reshape(prompts, seq_len, kv_local, HEAD_DIM), (0, 2, 1, 3))
        scores = jnp.einsum('bsgrd,bgtd->bgrst', queries, k_cache, preferred_element_type=jnp.float32) * HEAD_DIM ** -0.5
        positions = jnp.arange(seq_len)
        allowed = (positions[None, None, :] <= positions[None, :, None]) & (positions[None, None, :] < seq_lens[:, None, None])
        scores = jnp.where(allowed[:, None, None], scores, -1e30)
        attn_probs = jax.nn.softmax(scores, axis=-1).astype(jnp.bfloat16)
        attn_out = jnp.einsum('bgrst,bgtd->bsgrd', attn_probs, v_cache, preferred_element_type=jnp.float32).astype(jnp.bfloat16)
        attn_part = jnp.einsum('bsn,nd->bsd', attn_out.reshape(prompts, seq_len, -1), w_o, preferred_element_type=jnp.float32).astype(jnp.bfloat16)
        attn_proj = lax.psum(attn_part, 'tp')
        hidden = post_norm(tokens, attn_proj, g_attn)
        gate_pre = jnp.einsum('bsd,df->bsf', hidden, w_gate, preferred_element_type=jnp.float32)
        up_proj = jnp.einsum('bsd,df->bsf', hidden, w_up, preferred_element_type=jnp.float32)
        act_out = (jax.nn.silu(gate_pre) * up_proj).astype(jnp.bfloat16)
        mlp_part = jnp.einsum('bsf,fd->bsd', act_out, w_down, preferred_element_type=jnp.float32).astype(jnp.bfloat16)
        mlp_out = lax.psum(mlp_part, 'tp')
        out_hidden = post_norm(hidden, mlp_out, g_mlp)
        return out_hidden, k_cache, v_cache

    return jax.shard_map(local_layer, mesh=mesh, in_specs=(P('dp', None, None), P('dp'), P(None, 'tp'), P(None, 'tp'), P(None, 'tp'), P('tp', None), P('tp'), P('tp'), P(), P(), P(None, 'tp'), P(None, 'tp'), P('tp', None)), out_specs=(P('dp', None, None), P('dp', 'tp', None, None), P('dp', 'tp', None, None)), check_vma=False)
```

profile of v0, /device:TPU:0, one launch (start us, length us, event | category | flops | bytes accessed | tf_op | source)
XLA Modules:
  0.0 144.4 jit_solution(11599111947151438221)
XLA Ops:
  7.2 0.0 all-reduce.4.cloned.1.call-start
  7.2 0.0 copy-start
  7.3 0.0 copy-start.1
  7.3 5.2 %multiply_reduce_fusion.1 = (f32[2,64]{1,0:T(2,128)S(1)}, f32[2,64,1024]{2,1,0:T(8,128)S(1)}) fusion(bf16[2,64,4096]{2,1,0:T(8,128)(2,1)} %param.13, bf16[4096,1024]{1,0:T(8,128)(2,1)} %param.16), kind=kOutput, calls=%fused_computation.60 | convolution fusion | flops 1074003840 | bytes 9961984 | tf_op jit(solution)/shard_map/bsd,dn->bsn/dot_general | solution.py:43
  12.4 0.0 copy-done
  12.5 1.2 copy-done.1
  13.7 0.0 copy-start.7
  13.7 1.4 multiply_reduce_fusion
  15.1 0.0 copy-done.7
  15.1 0.0 copy-start.8
  15.1 8.7 %all-reduce = (f32[2,64,1]{1,0,2:T(2,128)S(1)}, f32[2,64,1]{1,0,2:T(2,128)S(1)}) all-reduce(f32[2,64,1]{1,0,2:T(2,128)S(1)} %bitcast.116, f32[2,64,1]{1,0,2:T(2,128)S(1)} %bitcast.117), channel_id=1, replica_groups=mesh['dp'=2,'tp'=4] {'tp'}, use_global_device_ids=true, to_apply=%region_1.0 | all-reduce | flops 256 | bytes 2048 | tf_op jit(solution)/shard_map/psum | solution.py:46
  23.9 0.1 copy_bitcast_fusion
  24.0 0.0 copy-start.2
  24.0 0.2 slice_negate_fusion
  24.2 0.2 fusion.64
  24.4 0.0 copy-done.8
  24.5 0.1 multiply_multiply_fusion
  24.6 0.1 copy.39
  24.7 0.0 copy-start.9
  24.7 0.2 fusion.67
  24.9 0.1 copy.52
  25.0 0.1 fusion.55
  25.1 0.5 copy-done.9
  25.6 0.1 iota_compare_fusion.1
  25.7 1.7 %copy-done.2 = bf16[4096,1024]{1,0:T(8,128)(2,1)S(1)} copy-done((bf16[4096,1024]{1,0:T(8,128)(2,1)S(1)}, bf16[4096,1024]{1,0:T(8,128)(2,1)}, u32[]{:S(2)}) %copy-start.2) | copy-done | bytes 8388632
  27.4 1.3 fusion.47
  28.7 0.1 copy.53
  28.8 0.0 copy-start.4
  28.8 0.1 broadcast_and_fusion
  28.9 0.2 fusion.57
  29.1 0.0 copy-start.3
  29.2 0.4 fusion.68
  29.6 0.1 fusion.56
  29.7 0.0 copy-done.4
  29.7 0.3 fusion.46
  30.0 0.0 copy-done.3
  30.0 0.2 copy.32
  30.2 0.1 reshape.207
  30.3 0.0 copy-start.5
  30.3 5.6 %fusion.14 = bf16[2,64,4096]{2,1,0:T(8,128)(2,1)} fusion(bf16[2,64,1024]{2,1,0:T(8,128)(2,1)S(1)} %reshape.207, bf16[1024,4096]{1,0:T(8,128)(2,1)} %param.18), kind=kOutput, calls=%fused_computation.14 | convolution fusion | flops 1074266112 | bytes 9699328 | tf_op jit(solution)/shard_map/bsn,nd->bsd/dot_general | solution.py:60
  35.9 0.0 all-reduce.4.cloned.1.call-update
  36.0 0.2 all-reduce.6.cloned.1.call-start
  36.2 0.0 copy-done.5
  36.2 30.8 %all-reduce.4.cloned.1.call-done = bf16[2,64,4096]{2,1,0:T(8,128)(2,1)} async-done(((bf16[2,64,4096]{2,1,0:T(8,128)(2,1)}), bf16[2,64,4096]{2,1,0:T(8,128)(2,1)}) %all-reduce.4.cloned.1.call-update) | async-done | bytes 1048592 | tf_op jit(solution)/shard_map/psum | solution.py:61
  67.0 1.5 %fusion.28 = f32[2,64]{1,0:T(2,128)S(1)} fusion(bf16[2,64,4096]{2,1,0:T(8,128)(2,1)} %all-reduce.4.cloned.1.call-done), kind=kLoop, calls=%fused_computation.22 | loop fusion | flops 1572736 | bytes 1049088 | tf_op jit(solution)/shard_map/reduce_sum | solution.py:27
  68.5 1.7 %fusion.31 = bf16[2,64,4096]{2,1,0:T(8,128)(2,1)S(1)} fusion(bf16[2,64,4096]{2,1,0:T(8,128)(2,1)} %all-reduce.4.cloned.1.call-done, bf16[2,64,4096]{2,1,0:T(8,128)(2,1)S(1)} %copy-done, f32[4096]{0:T(1024)S(1)} %convert_element_type.75, f32[2,64]{1,0:T(2,128)S(1)} %add_rsqrt_fusion.1), kind=kLoop, calls=%fused_computation.25 | loop fusion | flops 3145728 | bytes 3162624 | tf_op jit(solution)/shard_map/convert_element_type | solution.py:32
  70.2 12.0 %fusion.4 = f32[2,64,2752]{2,1,0:T(8,128)S(1)} fusion(bf16[2,64,4096]{2,1,0:T(8,128)(2,1)S(1)} %fusion.31, bf16[4096,2752]{0,1:T(8,128)(2,1)} %param.23), kind=kOutput, calls=%fused_computation.4 | convolution fusion | flops 2885681152 | bytes 25001984 | tf_op jit(solution)/shard_map/bsd,df->bsf/dot_general | solution.py:63
  82.2 0.0 copy-start.6
  82.2 19.9 %fusion.17 = bf16[2,64,4096]{2,1,0:T(8,128)(2,1)} fusion(bf16[2752,4096]{1,0:T(8,128)(2,1)} %param.25, bf16[2,64,4096]{2,1,0:T(8,128)(2,1)S(1)} %fusion.31, bf16[4096,2752]{0,1:T(8,128)(2,1)} %param.24, f32[2,64,2752]{2,1,0:T(8,128)S(1)} %fusion.4), kind=kOutput, calls=%fused_computation.15 | convolution fusion | flops 5774000128 | bytes 48594944 | tf_op jit(solution)/shard_map/bsf,fd->bsd/dot_general | solution.py:66
  102.1 0.0 all-reduce.6.cloned.1.call-update
  102.1 0.0 copy-done.6
  102.1 31.2 %all-reduce.6.cloned.1.call-done = bf16[2,64,4096]{2,1,0:T(8,128)(2,1)} async-done(((bf16[2,64,4096]{2,1,0:T(8,128)(2,1)}), bf16[2,64,4096]{2,1,0:T(8,128)(2,1)}) %all-reduce.6.cloned.1.call-update) | async-done | bytes 1048592 | tf_op jit(solution)/shard_map/psum | solution.py:67
  133.3 1.5 %fusion.32 = f32[2,64]{1,0:T(2,128)S(1)} fusion(bf16[2,64,4096]{2,1,0:T(8,128)(2,1)} %all-reduce.6.cloned.1.call-done), kind=kLoop, calls=%fused_computation.26 | loop fusion | flops 1572736 | bytes 1049088 | tf_op jit(solution)/shard_map/reduce_sum | solution.py:27
  134.9 2.7 %fusion.35 = bf16[2,64,4096]{2,1,0:T(8,128)(2,1)} fusion(bf16[2,64,4096]{2,1,0:T(8,128)(2,1)} %all-reduce.6.cloned.1.call-done, bf16[2,64,4096]{2,1,0:T(8,128)(2,1)S(1)} %fusion.31, f32[4096]{0:T(1024)S(1)} %convert_element_type.81, f32[2,64]{1,0:T(2,128)S(1)} %add_rsqrt_fusion), kind=kLoop, calls=%fused_computation.29 | loop fusion | flops 3145728 | bytes 3162624 | tf_op jit(solution)/shard_map/convert_element_type | solution.py:32
  (10 shorter events, 0.1 us)
Async XLA Ops:
  7.2 59.8 %all-reduce.4.cloned.1.call-start = ((), (), s32[]{:S(2)}) async-start(), calls=%async_computation | async-start | bytes 2097152 | tf_op jit(solution)/shard_map/psum | solution.py:61
  7.2 5.2 %copy-start = (bf16[2,64,4096]{2,1,0:T(8,128)(2,1)S(1)}, bf16[2,64,4096]{2,1,0:T(8,128)(2,1)}, u32[]{:S(2)}) copy-start(bf16[2,64,4096]{2,1,0:T(8,128)(2,1)} %param.13) | copy-start | bytes 3145732
  7.3 6.4 %copy-start.1 = (bf16[4096,1024]{1,0:T(8,128)(2,1)S(1)}, bf16[4096,1024]{1,0:T(8,128)(2,1)}, u32[]{:S(2)}) copy-start(bf16[4096,1024]{1,0:T(8,128)(2,1)} %param.15) | copy-start | bytes 25165828
  13.7 1.4 copy-start.7
  15.1 9.4 %copy-start.8 = (bf16[1024]{0:T(1024)(128)(2,1)S(1)}, bf16[1024]{0:T(1024)(128)(2,1)}, u32[]{:S(2)}) copy-start(bf16[1024]{0:T(1024)(128)(2,1)} %param.19) | copy-start | bytes 6148
  24.0 3.4 %copy-start.2 = (bf16[4096,1024]{1,0:T(8,128)(2,1)S(1)}, bf16[4096,1024]{1,0:T(8,128)(2,1)}, u32[]{:S(2)}) copy-start(bf16[4096,1024]{1,0:T(8,128)(2,1)} %param.17) | copy-start | bytes 25165828
  24.7 0.9 copy-start.9
  28.8 0.9 copy-start.4
  29.1 0.8 copy-start.3
  30.3 5.9 %copy-start.5 = (bf16[4096]{0:T(1024)(128)(2,1)S(1)}, bf16[4096]{0:T(1024)(128)(2,1)}, u32[]{:S(2)}) copy-start(bf16[4096]{0:T(1024)(128)(2,1)} %param.21) | copy-start | bytes 24580
  36.0 97.4 %all-reduce.6.cloned.1.call-start = ((), (), s32[]{:S(2)}) async-start(), calls=%async_computation.1 | async-start | bytes 2097152 | tf_op jit(solution)/shard_map/psum | solution.py:67
  82.2 19.9 %copy-start.6 = (bf16[4096]{0:T(1024)(128)(2,1)S(1)}, bf16[4096]{0:T(1024)(128)(2,1)}, u32[]{:S(2)}) copy-start(bf16[4096]{0:T(1024)(128)(2,1)} %param.22) | copy-start | bytes 24580
Sparse Core Ops, SparseCore 0:
  36.1 30.8 all-reduce.3
  102.2 31.0 all-reduce.5
where the time goes:
time: 145 us; the launch traced here: 144 us
  waiting for transfers between devices  62 us (43%)
  matrix products  46.1 us (32%)
  between operations  14.3 us (10%)
  blocking collectives  8.75 us (6%)
  other arithmetic  8.71 us (6%)
  local copies, waits for them, and re-layouts  4.2 us (3%)
    psum x1, waiting for transfers between devices, local_layer(): mlp_out = lax.psum(mlp_part, 'tp')  31.2 us
    psum x1, waiting for transfers between devices, local_layer(): attn_proj = lax.psum(attn_part, 'tp')  30.8 us
    dot_general x1, matrix products, local_layer(): jnp.einsum('bsf,fd->bsd', act_out, w_down, preferred_element_type=jnp.flo...  19.9 us
    dot_general x1, matrix products, local_layer(): jnp.einsum('bsd,df->bsf', hidden, w_gate, preferred_element_type=jnp.floa...  12 us
    psum x1, blocking collectives, local_layer(): k_sumsq = lax.psum(jnp.sum(k_raw * k_raw, axis=-1, keepdims=True), 'tp')  8.75 us
    dot_general x1, matrix products, local_layer(): jnp.einsum('bsn,nd->bsd', attn_out.reshape(prompts, seq_len, -1), w_o, pr...  5.62 us
    dot_general x1, matrix products, local_layer(): jnp.einsum('bsd,dn->bsn', tokens, w_k, preferred_element_type=jnp.float32)  5.18 us
    convert_element_type x2, other arithmetic, post_norm(): (base.astype(jnp.float32) + branch32 * rms_scale(branch32) * gain.astype(...  4.33 us
  transfers between devices with their start and end apart: 2, of which 2 were waited for; matrix products, arithmetic and copies ran while one was open for 0% of the time, Pallas kernels for 0%

commit v1 on v0

v1 whole, which is shorter than its diff:
```python
import functools

import jax
import jax.numpy as jnp
import numpy as np
from jax import lax
from jax.experimental import pallas as pl
from jax.experimental.pallas import tpu as pltpu
from jax.sharding import PartitionSpec as P

HEAD_DIM = 128
ROPE_BASE = 500000.0
NORM_EPS = 1e-6

SEQ = 64
PROMPTS = 2
ROWS = SEQ * PROMPTS
HALF = ROWS // 2
D = 4096
QW = 1024
HEADS = QW // HEAD_DIM
FF = 2752
FFP = 2816
KC = 1024
CW = 512
NC = D // CW
TB = 256
NTB = FFP // TB
NS = 4
NT = 512

F32 = jnp.float32
BF16 = jnp.bfloat16
MESH = pl.DeviceIdType.MESH


def rope_tables():
    half = HEAD_DIM // 2
    inv_freq = ROPE_BASE ** (-2.0 * np.arange(half, dtype=np.float64) / HEAD_DIM)
    inv_freq = inv_freq.astype(np.float32)
    angles = np.arange(SEQ, dtype=np.float32)[:, None] * inv_freq[None, :]
    cos = np.cos(angles.astype(np.float64)).astype(np.float32)
    sin = np.sin(angles.astype(np.float64)).astype(np.float32)
    cos2 = np.concatenate([cos, cos], axis=1)
    sin2 = np.concatenate([-sin, sin], axis=1)
    return np.stack([np.tile(cos2, (PROMPTS, 1)), np.tile(sin2, (PROMPTS, 1))])


def dot(a, b):
    return jnp.dot(a, b, preferred_element_type=F32)


def kernel(lens, tok, wq, wk, wv, wo, gq_h, gk_h, ga_h, gm_h, wg, wu, wd, tab_h,
           y_h, kc_h, vc_h,
           stg, wgu, xh, acc, kout, vout, ob, part, d2d, xsend, xrecv, full, act,
           tab, gq, gk, ga, gm, ga32, gm32, st, st_recv, ssq,
           sem_in, sem_r, sem_g, sem_d, sem_out, st_s, st_r,
           d_s, d_r, x_s, x_r, a_s, a_r):
    me = lax.axis_index("tp")
    core = lax.rem(me, 2)
    partner = me + 1 - 2 * core
    cross = lax.rem(me + 2, 4)
    mine = pl.ds(pl.multiple_of(core * HALF, HALF), HALF)
    theirs = pl.ds(pl.multiple_of((1 - core) * HALF, HALF), HALF)
    local = pltpu.make_async_copy

    small = [(tok, xh), (tab_h, tab), (gq_h, gq), (gk_h, gk), (ga_h, ga), (gm_h, gm)]

    def in_copy(i):
        return local(small[i][0], small[i][1], sem_in.at[i])

    def slot(i):
        i = i % 8
        return wgu.at[1, pl.ds((i % 4) * KC, KC), pl.ds((i // 4) * KC, KC)]

    qkv = [wq, wk, wv]

    def stream(i):
        if i < 12:
            src = qkv[i // 4].at[pl.ds((i % 4) * KC, KC), :]
        else:
            src = wo.at[:, pl.ds((i - 12) * KC, KC)]
        return local(src, slot(i), sem_r.at[i])

    def gu_copy(w, n, s):
        rows = TB if n < NTB - 1 else FF - TB * (NTB - 1)
        return local(w.at[pl.ds(n * TB, rows), :], stg.at[s, pl.ds(0, rows), :], sem_g.at[s])

    def gu_start(j):
        s = lax.rem(j, NS)
        n = lax.rem(j, NTB)
        for m, w in enumerate((wg, wu)):
            @pl.when((j // NTB == m) & (n < NTB - 1))
            def _():
                rows = pl.ds(pl.multiple_of(n * TB, TB), TB)
                local(w.at[rows, :], stg.at[s], sem_g.at[s]).start()

            @pl.when((j // NTB == m) & (n == NTB - 1))
            def _():
                gu_copy(w, NTB - 1, s).start()

    def gu_wait(j):
        s = lax.rem(j, NS)
        n = lax.rem(j, NTB)

        @pl.when(n < NTB - 1)
        def _():
            gu_copy(wg, 0, s).wait()

        @pl.when(n == NTB - 1)
        def _():
            gu_copy(wg, NTB - 1, s).wait()

    def down_cols(c):
        return pl.ds(pl.multiple_of(c // 2 * CW, CW), CW)

    def down_copy(c):
        return local(wd.at[:, pl.ds(pl.multiple_of(c * CW, CW), CW)],
                     wgu.at[lax.rem(c, 2), pl.ds(0, FF), down_cols(c)], sem_d.at[c])

    in_copy(0).start()
    stream(0).start()
    for i in range(1, 6):
        in_copy(i).start()
    for i in range(1, 8):
        stream(i).start()

    barrier = pltpu.get_barrier_semaphore()
    for j in range(1, 4):
        pl.semaphore_signal(barrier, inc=1, device_id={"tp": lax.rem(me + j, 4)}, device_id_type=MESH)
    acc[...] = jnp.zeros_like(acc)
    st[...] = jnp.zeros_like(st)
    act[:, FF // 128 * 128:] = jnp.zeros((ROWS, FFP - FF // 128 * 128), BF16)
    in_copy(0).wait()

    def qkv_step(i):
        stream(i).wait()
        w, k = i // 4, i % 4
        acc[w] += dot(xh[:, k * KC:(k + 1) * KC], slot(i)[...])
        if i + 8 < 16:
            stream(i + 8).start()

    for i in range(8):
        qkv_step(i)
    for j in range(NS):
        gu_copy(wg, j, j).start()

    for w in range(2):
        t = jnp.zeros((ROWS, 128), F32)
        for h in range(HEADS):
            v = acc[w, :, h * 128:(h + 1) * 128]
            t = t + v * v
        st[w:w + 1, :] = jnp.sum(t.T, axis=0, keepdims=True)
    pl.semaphore_wait(barrier, 3)

    def st_copy(j):
        return pltpu.make_async_remote_copy(
            st, st_recv.at[j - 1], st_s.at[j - 1], st_r.at[j - 1],
            device_id={"tp": lax.rem(me + j, 4)}, device_id_type=MESH)

    for j in range(1, 4):
        st_copy(j).start()
    for i in range(8, 12):
        qkv_step(i)
    for i in range(1, 6):
        in_copy(i).wait()
    ga32[...] = ga[...].astype(F32)
    gm32[...] = gm[...].astype(F32)
    gq32, gk32 = gq[...].astype(F32), gk[...].astype(F32)
    for h in range(HEADS):
        vh = acc[2, :, h * 128:(h + 1) * 128].astype(BF16)
        vout[0, h] = vh[:SEQ]
        vout[1, h] = vh[SEQ:]
    v_out = local(vout, vc_h, sem_out.at[0])
    v_out.start()
    for j in range(1, 4):
        st_copy(j).wait()

    tot = st[...] + st_recv[0] + st_recv[1] + st_recv[2]
    rs = lax.rsqrt(tot * (1.0 / D) + NORM_EPS)
    rq = jnp.broadcast_to(rs[0:1, :], (ROWS, 128)).T
    rk = jnp.broadcast_to(rs[1:2, :], (ROWS, 128)).T
    cos, sin = tab[0], tab[1]

    def rope(v):
        return v * cos + pltpu.roll(v, 64, axis=1) * sin

    ri = lax.broadcasted_iota(jnp.int32, (ROWS, ROWS), 0)
    ci = lax.broadcasted_iota(jnp.int32, (ROWS, ROWS), 1)
    same = (ri < SEQ) == (ci < SEQ)
    limit = jnp.where(ci < SEQ, lens[0], lens[1] + SEQ)
    allowed = same & (ci <= ri) & (ci < limit)
    for h in range(HEADS):
        cols = slice(h * 128, (h + 1) * 128)
        qh = rope(acc[0, :, cols] * rq * gq32[h:h + 1]).astype(BF16)
        kh = rope(acc[1, :, cols] * rk * gk32[h:h + 1]).astype(BF16)
        kout[0, h] = kh[:SEQ]
        kout[1, h] = kh[SEQ:]
        s = lax.dot_general(qh, kh, (((1,), (1,)), ((), ())), preferred_element_type=F32) * HEAD_DIM ** -0.5
        s = jnp.where(allowed, s, -1e30)
        e = jnp.exp(s - jnp.max(s, axis=1, keepdims=True))
        p = (e / jnp.sum(e, axis=1, keepdims=True)).astype(BF16)
        vh = jnp.concatenate([vout[0, h], vout[1, h]], axis=0)
        ob[:, cols] = dot(p, vh).astype(BF16)
    k_out = local(kout, kc_h, sem_out.at[1])
    k_out.start()

    def d_copy(ph, c):
        return pltpu.make_async_remote_copy(
            part.at[c, theirs, :], d2d.at[c], d_s.at[ph, c], d_r.at[ph, c],
            device_id={"tp": partner}, device_id_type=MESH)

    def x_copy(ph, c):
        return pltpu.make_async_remote_copy(
            xsend.at[c], xrecv.at[ph, c], x_s.at[ph, c], x_r.at[ph, c],
            device_id={"tp": cross}, device_id_type=MESH)

    def cols_of(c):
        return pl.ds(pl.multiple_of(c * CW, CW), CW)

    def a_copy(ph, c):
        blk = full.at[mine, cols_of(c)]
        return pltpu.make_async_remote_copy(
            blk, blk, a_s.at[ph, c], a_r.at[ph, c],
            device_id={"tp": partner}, device_id_type=MESH)

    def put(ph, c, val):
        part[c] = val.astype(BF16)
        d_copy(ph, c).start()

    def relay(ph, c):
        d_copy(ph, c).wait()
        xsend[c] = (part[c, mine, :].astype(F32) + d2d[c].astype(F32)).astype(BF16)
        x_copy(ph, c).start()

    def add_sq(rows, c):
        v = full[rows, cols_of(c)].astype(F32)
        v = v * v
        t = v[:, 0:128]
        for q in range(1, CW // 128):
            t = t + v[:, q * 128:(q + 1) * 128]
        ssq[rows, :] += t

    def finish_own(ph, c):
        x_copy(ph, c).wait()
        s = xsend[c].astype(F32) + xrecv[ph, c].astype(F32)
        full[mine, cols_of(c)] = s.astype(BF16)
        a_copy(ph, c).start()
        add_sq(mine, c)

    def finish_other(ph, c):
        a_copy(ph, c).wait()
        add_sq(theirs, c)

    def norm(g32):
        rs = lax.rsqrt(jnp.sum(ssq[...], axis=1, keepdims=True) * (1.0 / D) + NORM_EPS)

        @pl.loop(0, NC)
        def _(c):
            for q in range(CW // 128):
                cols = pl.ds(pl.multiple_of(c * CW + q * 128, 128), 128)
                v = full[:, cols].astype(F32) * rs * g32[pl.ds(c * (CW // 128) + q, 1), :]
                xh[:, cols] = (xh[:, cols].astype(F32) + v).astype(BF16)

    ssq[...] = jnp.zeros_like(ssq)
    lag = 3
    for c in range(4):
        stream(12 + c).wait()
        for half in range(2):
            cc = 2 * c + half
            put(0, cc, dot(ob[...], slot(12 + c)[:, half * CW:(half + 1) * CW]))
            if cc >= lag:
                relay(0, cc - lag)

    @pl.loop(0, 2 * NTB)
    def _(j):
        gu_wait(j)
        s, m, n = lax.rem(j, NS), j // NTB, lax.rem(j, NTB)
        cols = pl.ds(pl.multiple_of(n * TB, TB), TB)
        wgu[m, :, cols] = stg[s].T

        @pl.when(j + NS < 2 * NTB)
        def _():
            gu_start(j + NS)

        @pl.when(j < lag)
        def _():
            relay(0, NC - lag + j)

        @pl.when((j >= 6) & (lax.rem(j, 2) == 0))
        def _():
            finish_own(0, (j - 6) // 2)

        @pl.when((j >= 7) & (lax.rem(j, 2) == 1))
        def _():
            finish_other(0, (j - 7) // 2)

    norm(ga32)

    def gate_up(start, width, keep):
        g = dot(xh[...], wgu[0, :, pl.ds(start, width)])
        u = dot(xh[...], wgu[1, :, pl.ds(start, width)])
        v = (g * jax.nn.sigmoid(g) * u).astype(BF16)
        act[:, pl.ds(start, keep)] = v[:, :keep]

    @pl.loop(0, FF // NT)
    def _(n):
        gate_up(pl.multiple_of(n * NT, NT), NT, NT)

        @pl.when(n < NC // 2)
        def _():
            down_copy(2 * n).start()
            down_copy(2 * n + 1).start()

    tail = FF // NT * NT
    gate_up(tail, FFP - tail, FF - tail)
    ssq[...] = jnp.zeros_like(ssq)

    lag2 = 2

    @pl.loop(0, NC)
    def _(c):
        down_copy(c).wait()
        put(1, c, dot(act[...], wgu[lax.rem(c, 2), :FFP, down_cols(c)]))

        @pl.when(c >= lag2)
        def _():
            relay(1, c - lag2)

    for cc in range(NC - lag2, NC):
        relay(1, cc)

    @pl.loop(0, NC)
    def _(c):
        finish_own(1, c)

        @pl.when(c > 0)
        def _():
            finish_other(1, c - 1)

    finish_other(1, NC - 1)
    norm(gm32)
    y_out = local(xh, y_h, sem_out.at[2])
    y_out.start()
    y_out.wait()
    v_out.wait()
    k_out.wait()


def solution(mesh):
    tables = rope_tables()

    def local_layer(tokens, seq_lens, w_q, w_k, w_v, w_o, g_q, g_k, g_attn, g_mlp, w_gate, w_up, w_down):
        anyspace = pl.BlockSpec(memory_space=pl.ANY)
        dma = pltpu.SemaphoreType.DMA
        y, kc, vc = pl.pallas_call(
            kernel,
            out_shape=(
                jax.ShapeDtypeStruct((ROWS, D), BF16),
                jax.ShapeDtypeStruct((PROMPTS, HEADS, SEQ, HEAD_DIM), BF16),
                jax.ShapeDtypeStruct((PROMPTS, HEADS, SEQ, HEAD_DIM), BF16),
            ),
            in_specs=[pl.BlockSpec(memory_space=pltpu.SMEM)] + [anyspace] * 13,
            out_specs=(anyspace,) * 3,
            scratch_shapes=[
                pltpu.VMEM((NS, TB, D), BF16),
                pltpu.VMEM((2, D, FFP), BF16),
                pltpu.VMEM((ROWS, D), BF16),
                pltpu.VMEM((3, ROWS, QW), F32),
                pltpu.VMEM((PROMPTS, HEADS, SEQ, HEAD_DIM), BF16),
                pltpu.VMEM((PROMPTS, HEADS, SEQ, HEAD_DIM), BF16),
                pltpu.VMEM((ROWS, QW), BF16),
                pltpu.VMEM((NC, ROWS, CW), BF16),
                pltpu.VMEM((NC, HALF, CW), BF16),
                pltpu.VMEM((NC, HALF, CW), BF16),
                pltpu.VMEM((2, NC, HALF, CW), BF16),
                pltpu.VMEM((ROWS, D), BF16),
                pltpu.VMEM((ROWS, FFP), BF16),
                pltpu.VMEM((2, ROWS, HEAD_DIM), F32),
                pltpu.VMEM((QW // 128, 128), BF16),
                pltpu.VMEM((QW // 128, 128), BF16),
                pltpu.VMEM((D // 128, 128), BF16),
                pltpu.VMEM((D // 128, 128), BF16),
                pltpu.VMEM((D // 128, 128), F32),
                pltpu.VMEM((D // 128, 128), F32),
                pltpu.VMEM((8, 128), F32),
                pltpu.VMEM((3, 8, 128), F32),
                pltpu.VMEM((ROWS, 128), F32),
                dma((6,)), dma((16,)), dma((NS,)), dma((NC,)), dma((3,)), dma((3,)), dma((3,)),
                dma((2, NC)), dma((2, NC)), dma((2, NC)), dma((2, NC)), dma((2, NC)), dma((2, NC)),
            ],
            compiler_params=pltpu.CompilerParams(
                collective_id=0, has_side_effects=True, vmem_limit_bytes=67043328),
            name="layer",
        )(seq_lens, tokens.reshape(ROWS, D), w_q, w_k, w_v, w_o,
          g_q.reshape(-1, 128), g_k.reshape(-1, 128), g_attn.reshape(-1, 128), g_mlp.reshape(-1, 128),
          w_gate.T, w_up.T, w_down, jnp.asarray(tables))
        return y.reshape(tokens.shape), kc, vc

    return jax.shard_map(local_layer, mesh=mesh, in_specs=(P('dp', None, None), P('dp'), P(None, 'tp'), P(None, 'tp'), P(None, 'tp'), P('tp', None), P('tp'), P('tp'), P(), P(), P(None, 'tp'), P(None, 'tp'), P('tp', None)), out_specs=(P('dp', None, None), P('dp', 'tp', None, None), P('dp', 'tp', None, None)), check_vma=False)
```

time: 145 us -> 68.1 us (0.47)
  waiting for transfers between devices: 62 us -> 0 us
  Pallas kernels: 0 us -> 61.6 us
  matrix products: 46.1 us -> 0 us
  between operations: 14.3 us -> 0.65 us
  blocking collectives: 8.75 us -> 0 us
  other arithmetic: 8.71 us -> 0 us
    psum x2 -> x0, waiting for transfers between devices: 62 us -> none  [the longest x1 31.2 us: local_layer(): mlp_out = lax.psum(mlp_part, 'tp')]
    pallas_call x0 -> x1, Pallas kernels: none -> 61.6 us  [local_layer(): pl.pallas_call(kernel, out_shape=(jax.ShapeDtypeStruct((ROWS, D), BF16),...]
    dot_general x8 -> x0, matrix products: 46.1 us -> none  [the longest x1 19.9 us: local_layer(): jnp.einsum('bsf,fd->bsd', act_out, w_down, preferred_element_type=jnp.flo...]
    psum x1 -> x0, blocking collectives: 8.75 us -> none  [local_layer(): k_sumsq = lax.psum(jnp.sum(k_raw * k_raw, axis=-1, keepdims=True), 'tp')]
    convert_element_type x6 -> x0, other arithmetic: 4.35 us -> none  [the longest x2 4.33 us: post_norm(): (base.astype(jnp.float32) + branch32 * rms_scale(branch32) * gain.astype(...]
    reduce_sum x3 -> x0, other arithmetic: 3.15 us -> none  [the longest x2 3.04 us: rms_scale(): return lax.rsqrt(jnp.mean(vals * vals, axis=-1, keepdims=True) + NORM_EPS)]
    unnamed x22 -> x3, local copies, waits for them, and re-layouts: 3.65 us -> 5.63 us
  transfers between devices with their start and end apart: 2 -> 0, of which waited for: 2 -> 0; matrix products, arithmetic and copies ran while one was open for 0% -> 0% of each run, Pallas kernels for 0% -> 0%
where the time goes in v1:
time: 68.1 us; the launch traced here: 67.8 us
  Pallas kernels  61.6 us (90%)
  local copies, waits for them, and re-layouts  5.63 us (8%)
    pallas_call x1, Pallas kernels, local_layer(): pl.pallas_call(kernel, out_shape=(jax.ShapeDtypeStruct((ROWS, D), BF16),...  61.6 us
    unnamed x3, local copies, waits for them, and re-layouts  5.63 us

profile of v1, /device:TPU:0, one launch (start us, length us, event | category | flops | bytes accessed | tf_op | source)
XLA Modules:
  0.0 67.8 jit_solution(3174556972068780344)
XLA Ops:
  0.6 61.6 %layer.1 = (bf16[128,4096]{1,0:T(8,128)(2,1)}, bf16[2,8,64,128]{3,2,1,0:T(8,128)(2,1)}, bf16[2,8,64,128]{3,2,1,0:T(8,128)(2,1)}) custom-call(s32[2]{0:T(128)} %lens.1, bf16[128,4096]{1,0:T(8,128)(2,1)} %bitcast.10, bf16[4096,1024]{1,0:T(8,128)(2,1)} %wq.1, bf16[4096,1024]{1,0:T(8,128)(2,1)} %wk.1, bf16[4096,1024]{1,0:T(8,128)(2,1)} %wv.1, ...), custom_call_target="tpu_custom_call" | custom-call | tf_op jit(solution)/shard_map/layer/pallas_call | solution.py:356
  62.2 2.3 %copy.20 = bf16[2,64,4096]{2,1,0:T(8,128)(2,1)} copy(bf16[2,64,4096]{2,1,0:T(8,128)(2,1)} %bitcast.11) | data formatting | bytes 2097152
  64.5 1.7 %copy.21 = bf16[2,8,64,128]{3,2,1,0:T(8,128)(2,1)} copy(bf16[2,8,64,128]{3,2,1,0:T(8,128)(2,1)} %get-tuple-element.13) | data formatting | bytes 524288
  66.2 1.7 %copy.22 = bf16[2,8,64,128]{3,2,1,0:T(8,128)(2,1)} copy(bf16[2,8,64,128]{3,2,1,0:T(8,128)(2,1)} %get-tuple-element.14) | data formatting | bytes 524288
